TPU v7x, 32 devices: a 4x4x1 block of a 4x4x8 slice. The times are simulated.
32 devices in a mesh: dp: 1 (over z), vp: 4 (over y), tp: 8 (over x, core).
Axes of the slice: x: 4, y: 4, z: 1, core: 2. Of those that a mesh axis runs over, the one named last changes fastest.
The devices are a block of a 4x4x8 slice.
Arguments:
- hidden: bfloat16 [64, 2048], P('dp', 'tp')
- lnf_gain: float32 [2048], P('tp')
- lnf_bias: float32 [2048], P('tp')
- emb_table: bfloat16 [250880, 2048], P('vp', 'tp')
- next_tok: int32 [64], P('dp')
- eln_gain: float32 [2048], P('tp')
- eln_bias: float32 [2048], P('tp')
Outputs:
- output 1: float32 [64, 250880], P('dp', ('vp', 'tp'))
- output 2: float32 [64], P('dp')
- output 3: bfloat16 [64, 2048], P('dp', 'tp')
All inputs are finite; a program needn't handle non-finite values.
Results may differ from a plain program's by a relative error of at most 0.001.
Values sent between devices are 32-bit elements.
A program may use at most 768 MiB of HBM per device.

v0:
```python
import jax
import jax.numpy as jnp
from jax import lax
from jax.sharding import PartitionSpec as P

NORM_EPS = 1e-5


def norm_shard(rows_in, norm_gain, norm_bias, full_width):
    rows_f32 = rows_in.astype(jnp.float32)
    row_sums = jnp.stack([jnp.sum(rows_f32, axis=1), jnp.sum(rows_f32 * rows_f32, axis=1)])
    row_sums = lax.psum(row_sums, "tp")
    row_mean = row_sums[0] / full_width
    row_var = row_sums[1] / full_width - row_mean * row_mean
    scaled = (rows_f32 - row_mean[:, None]) * lax.rsqrt(row_var + NORM_EPS)[:, None]
    return (scaled * norm_gain + norm_bias).astype(jnp.bfloat16)


def global_lse(logits):
    row_top = lax.pmax(jnp.max(logits, axis=1), ("vp", "tp"))
    exp_total = lax.psum(jnp.sum(jnp.exp(logits - row_top[:, None]), axis=1), ("vp", "tp"))
    return row_top + jnp.log(exp_total)


def solution(mesh):
    tp_size = mesh.shape["tp"]

    def per_device(hidden, lnf_gain, lnf_bias, emb_table, next_tok, eln_gain, eln_bias):
        full_width = hidden.shape[1] * tp_size
        normed = norm_shard(hidden, lnf_gain, lnf_bias, full_width)
        shard_logits = lax.dot_general(normed, emb_table, (((1,), (1,)), ((), ())), preferred_element_type=jnp.float32)
        logits = lax.psum_scatter(shard_logits, "tp", scatter_dimension=1, tiled=True)
        log_sum = global_lse(logits)
        logprobs = logits - log_sum[:, None]
        block_rows = emb_table.shape[0]
        local_idx = next_tok - lax.axis_index("vp") * block_rows
        is_owned = (local_idx >= 0) & (local_idx < block_rows)
        picked = jnp.take(emb_table, jnp.clip(local_idx, 0, block_rows - 1), axis=0).astype(jnp.float32)
        picked = jnp.where(is_owned[:, None], picked, jnp.zeros_like(picked))
        tok_rows = lax.psum(picked, "vp")
        next_in = norm_shard(tok_rows, eln_gain, eln_bias, full_width)
        return logprobs, log_sum, next_in

    return jax.shard_map(
        per_device,
        mesh=mesh,
        in_specs=(P("dp", "tp"), P("tp"), P("tp"), P("vp", "tp"), P("dp"), P("tp"), P("tp")),
        out_specs=(P("dp", ("vp", "tp")), P("dp"), P("dp", "tp")),
        check_vma=False,
    )
```

profile of v0, /device:TPU:97, one launch (start us, length us, event | category | flops | bytes accessed | tf_op | source)
XLA Modules:
  0.0 354.7 jit_solution(7498896295283912716)
XLA Ops:
  7.2 0.1 all-reduce.3.cloned.1.call-start
  7.2 0.7 compare_and_fusion
  7.9 3.4 gather_fusion
  11.3 0.7 convert_select_fusion
  12.0 0.1 all-reduce.3.cloned.1.call-update
  12.1 0.1 reduce-scatter.4.cloned.1.call-start
  12.2 0.9 convert_reduce_fusion
  13.0 36.6 %all-reduce.3.cloned.1.call-done = f32[64,256]{1,0:T(8,128)} async-done(((f32[64,256]{1,0:T(8,128)}), f32[64,256]{1,0:T(8,128)}) %all-reduce.3.cloned.1.call-update) | async-done | bytes 65552 | tf_op jit(solution)/shard_map/psum | solution.py:40
  49.7 0.9 fusion.14
  50.6 14.5 %all-reduce = (f32[2,64]{1,0:T(2,128)S(1)}, f32[2,64]{1,0:T(2,128)S(1)}) all-reduce(f32[2,64]{1,0:T(2,128)S(1)} %get-tuple-element.12, f32[2,64]{1,0:T(2,128)S(1)} %get-tuple-element.13), channel_id=1, replica_groups=mesh['dp'=1,'vp'=4,'tp'=8] {'tp'}, use_global_device_ids=true, to_apply=%region_2.0 | all-reduce | flops 256 | bytes 2048 | tf_op jit(solution)/shard_map/psum | solution.py:12
  65.1 25.5 %convolution_bitcast_fusion = f32[62720,64]{1,0:T(8,128)} fusion(bf16[62720,256]{1,0:T(8,128)(2,1)} %param.10, bf16[64,256]{1,0:T(8,128)(2,1)} %param.7, f32[256]{0:T(256)} %param.9, f32[256]{0:T(256)} %param.8, f32[64]{0:T(128)S(1)} %fusion.13, f32[64]{0:T(128)S(1)} %multiply_bitcast_fusion.1), kind=kOutput, calls=%fused_computation.1 | convolution fusion | flops 2055307264 | bytes 48204288
  90.7 0.0 copy-start
  90.7 0.0 copy-start.1
  90.7 0.0 copy-start.2
  90.7 0.1 reduce-scatter.4.cloned.1.call-update
  90.8 0.7 copy-done
  91.5 0.0 copy-done.1
  91.5 0.0 copy-done.2
  91.5 0.7 add_convert_fusion
  92.2 158.2 %reduce-scatter.4.cloned.1.call-done = f32[7840,64]{1,0:T(8,128)} async-done(((f32[62720,64]{1,0:T(8,128)}), f32[7840,64]{1,0:T(8,128)}) %reduce-scatter.4.cloned.1.call-update) | async-done | bytes 2007056
  250.4 3.2 bitcast_reduce_fusion
  253.6 45.8 %pmax.7 = f32[64]{0:T(128)S(1)} all-reduce(f32[64]{0:T(128)S(1)} %bitcast_reduce_fusion), channel_id=1, replica_groups=mesh['dp'=1,'vp'=4,'tp'=8] {'vp','tp'}, use_global_device_ids=true, to_apply=%region_5.0 | all-reduce | flops 64 | bytes 512 | tf_op jit(solution)/shard_map/pmax | solution.py:20
  299.4 2.7 copy.11
  302.2 0.5 exponential_reduce_fusion
  302.6 43.7 %psum.29 = f32[64]{0:T(128)S(1)} all-reduce(f32[64]{0:T(128)S(1)} %exponential_reduce_fusion), channel_id=1, replica_groups=mesh['dp'=1,'vp'=4,'tp'=8] {'vp','tp'}, use_global_device_ids=true, to_apply=%region_7.0 | all-reduce | flops 64 | bytes 512 | tf_op jit(solution)/shard_map/psum | solution.py:21
  346.3 0.0 copy-start.3
  346.3 1.5 broadcast_subtract_fusion
  347.8 0.0 copy-done.3
  (7 shorter events, 0.0 us)
Async XLA Ops:
  7.2 42.5 %all-reduce.3.cloned.1.call-start = ((), (), s32[]{:S(2)}) async-start(), calls=%async_computation.1 | async-start | bytes 131072 | tf_op jit(solution)/shard_map/psum | solution.py:40
  12.1 238.3 %reduce-scatter.4.cloned.1.call-start = ((), (), s32[]{:S(2)}) async-start(), calls=%async_computation.2 | async-start | bytes 36126720
  90.7 0.8 copy-start
  90.7 0.8 copy-start.1
  90.7 0.8 copy-start.2
  346.3 1.5 copy-start.3
Sparse Core Ops, SparseCore 0:
  12.2 37.4 all-reduce.2
  90.9 159.5 reduce-scatter.3
where the time goes:
time: 355 us
  waiting for transfers between devices  195 us (55%)
  blocking collectives  104 us (29%)
  matrix products  25.5 us (7%)
  between operations  14.1 us (4%)
  other arithmetic  9.1 us (3%)
  local copies, waits for them, and re-layouts  6.89 us (2%)
    unnamed x3, waiting for transfers between devices  158 us
    pmax x1, blocking collectives, global_lse(): row_top = lax.pmax(jnp.max(logits, axis=1), ('vp', 'tp'))  45.8 us
    psum x1, blocking collectives, global_lse(): lax.psum(jnp.sum(jnp.exp(logits - row_top[:, None]), axis=1), ('vp', 'tp'))  43.7 us
    psum x1, waiting for transfers between devices, per_device(): tok_rows = lax.psum(picked, 'vp')  36.6 us
    unnamed x1, matrix products  25.5 us
    psum x1, blocking collectives, norm_shard(): row_sums = lax.psum(row_sums, 'tp')  14.5 us
  transfers between devices with their start and end apart: 2, of which 2 were waited for; matrix products, arithmetic and copies ran while one was open for 0% of the time, Pallas kernels for 0%

commit v1 on v0

v1 whole, which is shorter than its diff:
```python
import functools

import jax
import jax.numpy as jnp
from jax import lax
from jax.experimental import pallas as pl
from jax.experimental.pallas import tpu as pltpu
from jax.sharding import PartitionSpec as P

NORM_EPS = 1e-5
LANES = 128
CHUNK = 1024
DOT_COLS = 512
PICK = 1280
MESH_ID = pl.DeviceIdType.MESH


def _row_stats(x):
    sums = x[:, :LANES]
    squares = sums * sums
    for c in range(LANES, x.shape[1], LANES):
        part = x[:, c : c + LANES]
        sums = sums + part
        squares = squares + part * part
    both = jnp.concatenate([sums, squares], axis=0)
    return jnp.sum(both.T, axis=0, keepdims=True)


def _as_columns(row):
    return jnp.broadcast_to(row, (LANES, LANES)).T


def _normalize(x, total, gain, bias, full_width):
    rows = x.shape[0]
    cols = _as_columns(total)
    mean = cols[:rows] / full_width
    var = cols[rows : 2 * rows] / full_width - mean * mean
    rstd = lax.rsqrt(var + NORM_EPS)
    parts = []
    for c in range(0, x.shape[1], LANES):
        scaled = (x[:, c : c + LANES] - mean) * rstd
        parts.append(scaled * gain[:, c : c + LANES] + bias[:, c : c + LANES])
    return jnp.concatenate(parts, axis=1).astype(jnp.bfloat16)


def _head_kernel(
    tp_size, vp_size,
    hid, g1, b1, g2, b2, tok, emb,
    z_out, ls_out, nin_out,
    e_all, mine, from_peer, to_peer, ring, xn,
    top, acc, e_src, e_in, stat_src, stat_in, v_src, v_in,
    e_sem, peer_send, peer_recv, ring_send, ring_recv,
    stat_send, stat_recv, row_send, row_recv, v_send, v_recv, z_sem,
):
    rows, width = hid.shape
    full_width = width * tp_size
    vocab_rows = emb.shape[0]
    own_cols = vocab_rows // tp_size
    chips = tp_size // 2
    n_chunks = pl.cdiv(own_cols, CHUNK)
    half_chunks = n_chunks // 2
    half_cols = half_chunks * CHUNK
    tail = own_cols - (n_chunks - 1) * CHUNK
    tail_pad = pl.cdiv(tail, LANES) * LANES

    me = lax.axis_index("tp")
    my_vp = lax.axis_index("vp")
    chip = me // 2
    core = me % 2
    peer = 2 * chip + 1 - core
    turn = 1 - 2 * core

    def chip_at(offset):
        return (chip + offset + chips) % chips

    fwd = 2 * chip_at(turn) + core
    bwd = 2 * chip_at(-turn) + core

    barrier = pltpu.get_barrier_semaphore()
    for j in range(1, tp_size):
        pl.semaphore_signal(barrier, inc=1, device_id={"tp": (me + j) % tp_size}, device_id_type=MESH_ID)
    for j in range(1, vp_size):
        pl.semaphore_signal(barrier, inc=1, device_id={"vp": (my_vp + j) % vp_size}, device_id_type=MESH_ID)

    def block_of(phase, half, sign):
        if phase == 0:
            return chip_at(2)
        if phase == 3:
            return chip
        if (phase == 1) == (half == 0):
            return chip_at(-sign)
        return chip_at(sign)

    def first_row(phase, half, own):
        if own:
            return (2 * block_of(phase, half, turn) + core) * own_cols + half * half_cols
        return (2 * block_of(phase, half, -turn) + 1 - core) * own_cols + half * half_cols

    def table_load(phase, half, own):
        count = half_cols if half == 0 else own_cols - half_cols
        span = pl.ds(pl.multiple_of(first_row(phase, half, own), 16), count)
        return pltpu.make_async_copy(emb.at[span], e_all.at[span], e_sem.at[phase * 4 + half * 2 + own])

    for phase in range(4):
        for own in range(2):
            for half in range(2):
                table_load(phase, half, own).start()

    def stat_copy(s, j):
        return pltpu.make_async_remote_copy(
            src_ref=stat_src.at[s], dst_ref=stat_in.at[s, j - 1],
            send_sem=stat_send.at[s, j - 1], recv_sem=stat_recv.at[s, j - 1],
            device_id={"tp": (me + j) % tp_size}, device_id_type=MESH_ID)

    def vp_copy(src, dst, send, recv, j):
        return pltpu.make_async_remote_copy(
            src_ref=src, dst_ref=dst.at[j - 1], send_sem=send.at[j - 1], recv_sem=recv.at[j - 1],
            device_id={"vp": (my_vp + j) % vp_size}, device_id_type=MESH_ID)

    def stat_total(s):
        total = stat_src[s]
        for j in range(1, tp_size):
            stat_copy(s, j).wait()
            total = total + stat_in[s, j - 1]
        return total[:1]

    x = hid[...].astype(jnp.float32)
    stat_src[0] = jnp.broadcast_to(_row_stats(x), (8, LANES))
    pl.semaphore_wait(barrier, tp_size - 1 + vp_size - 1)
    for j in range(1, tp_size):
        stat_copy(0, j).start()
    xn[...] = _normalize(x, stat_total(0), g1[...], b1[...], full_width)

    def chunk_dot(dst, row0, cols):
        for c in range(0, cols, DOT_COLS):
            n = min(DOT_COLS, cols - c)
            part = e_all[pl.ds(pl.multiple_of(row0 + c, 16), n), :]
            dst[:, c : c + n] = lax.dot_general(
                xn[...], part, (((1,), (1,)), ((), ())), preferred_element_type=jnp.float32)
        if cols % LANES:
            end = pl.cdiv(cols, LANES) * LANES
            dst[:, cols:end] = jnp.zeros((rows, end - cols), jnp.float32)

    def cols_of(half, last):
        return (tail, tail_pad) if half == 1 and last else (CHUNK, CHUNK)

    def peer_copy(phase, half, k, last):
        lanes = pl.ds(0, cols_of(half, last)[1])
        slot, at = half * half_chunks + k, phase * n_chunks + half * half_chunks + k
        return pltpu.make_async_remote_copy(
            src_ref=to_peer.at[slot, :, lanes], dst_ref=from_peer.at[at, :, lanes],
            send_sem=peer_send.at[slot], recv_sem=peer_recv.at[at],
            device_id={"tp": peer}, device_id_type=MESH_ID)

    def ring_copy(phase, half, k, last):
        lanes = pl.ds(0, cols_of(half, last)[1])
        at = phase * n_chunks + half * half_chunks + k
        forward = (half == 0) != (phase == 1)
        return pltpu.make_async_remote_copy(
            src_ref=mine.at[at, :, lanes], dst_ref=ring.at[at, :, lanes],
            send_sem=ring_send.at[at], recv_sem=ring_recv.at[at],
            device_id={"tp": fwd if forward else bwd}, device_id_type=MESH_ID)

    def at_of(phase, half, k):
        return phase * n_chunks + half * half_chunks + k

    def add_into(at, others, width_):
        for r in range(0, rows, 8):
            v = mine[at, r : r + 8, :width_]
            for ref, i in others:
                v = v + ref[i, r : r + 8, :width_]
            mine[at, r : r + 8, :width_] = v

    def product(phase, k, last):
        for half in range(2):
            if phase:
                peer_copy(phase - 1, half, k, last).wait_send()
            chunk_dot(to_peer.at[half * half_chunks + k], first_row(phase, half, 0) + k * CHUNK, cols_of(half, last)[0])
        for half in range(2):
            peer_copy(phase, half, k, last).start()
        for half in range(2):
            chunk_dot(mine.at[at_of(phase, half, k)], first_row(phase, half, 1) + k * CHUNK, cols_of(half, last)[0])
        if phase < 2:
            for half in range(2):
                at = at_of(phase, half, k)
                peer_copy(phase, half, k, last).wait_recv()
                add_into(at, [(from_peer, at)], cols_of(half, last)[1])
            for half in range(2):
                ring_copy(phase, half, k, last).start()

    def each_chunk(body):
        def step(k, carry):
            body(k, False)
            return carry

        lax.fori_loop(0, half_chunks - 1, step, 0)
        body(half_chunks - 1, True)

    def wait_table(phase):
        for own in range(2):
            for half in range(2):
                table_load(phase, half, own).wait()

    wait_table(0)
    each_chunk(functools.partial(product, 0))

    for phase in range(1, 4):
        wait_table(phase)

    def pick_rows():
        wanted = tok[...].astype(jnp.float32) - (my_vp * vocab_rows).astype(jnp.float32)
        wanted = jnp.concatenate([wanted, jnp.zeros((1, LANES - rows), jnp.float32)], axis=1)
        wanted = _as_columns(wanted)[:rows].astype(jnp.int32)
        lane = lax.broadcasted_iota(jnp.int32, wanted.shape, 1)

        def add(first, count):
            hits = []
            for c in range(0, count, LANES):
                hits.append(jnp.where(lane + (first + c) == wanted, 1.0, 0.0).astype(jnp.bfloat16))
            e_src[...] += jnp.dot(
                jnp.concatenate(hits, axis=1), e_all[pl.ds(pl.multiple_of(first, LANES), count), :],
                preferred_element_type=jnp.float32)

        def step(i, carry):
            add(i * PICK, PICK)
            return carry

        e_src[...] = jnp.zeros_like(e_src)
        lax.fori_loop(0, vocab_rows // PICK, step, 0)
        if vocab_rows % PICK:
            add(vocab_rows // PICK * PICK, vocab_rows % PICK)

    each_chunk(functools.partial(product, 1))
    pick_rows()
    for j in range(1, vp_size):
        vp_copy(e_src, e_in, row_send, row_recv, j).start()
    each_chunk(functools.partial(product, 2))
    e_row = e_src[...]
    for j in range(1, vp_size):
        vp_copy(e_src, e_in, row_send, row_recv, j).wait()
        e_row = e_row + e_in[j - 1]
    stat_src[1] = jnp.broadcast_to(_row_stats(e_row), (8, LANES))
    for j in range(1, tp_size):
        stat_copy(1, j).start()

    def forward_chunk(k, last):
        for half in range(2):
            at = at_of(2, half, k)
            peer_copy(2, half, k, last).wait_recv()
            ring_copy(0, half, k, last).wait_recv()
            add_into(at, [(from_peer, at), (ring, at_of(0, half, k))], cols_of(half, last)[1])
        for half in range(2):
            ring_copy(2, half, k, last).start()

    each_chunk(forward_chunk)
    each_chunk(functools.partial(product, 3))

    e_row = e_src[...]
    for j in range(1, vp_size):
        e_row = e_row + e_in[j - 1]
    nin_out[...] = _normalize(e_row, stat_total(1), g2[...], b2[...], full_width)

    top[...] = jnp.full(top.shape, jnp.finfo(jnp.float32).min, jnp.float32)
    acc[...] = jnp.zeros_like(acc)

    def z_copy(half, k, last):
        n = cols_of(half, last)[1]
        off = pl.multiple_of((half * half_chunks + k) * CHUNK, LANES)
        return pltpu.make_async_copy(
            mine.at[at_of(3, half, k), :, pl.ds(0, n)], z_out.at[:, pl.ds(off, n)],
            z_sem.at[half * half_chunks + k])

    def finish_chunk(k, last):
        for half in range(2):
            at = at_of(3, half, k)
            real, padded = cols_of(half, last)
            peer_copy(3, half, k, last).wait_recv()
            ring_copy(1, half, k, last).wait_recv()
            ring_copy(2, half, k, last).wait_recv()
            for r in range(0, rows, 8):
                group = slice(r, r + 8)
                tiles = []
                for c in range(0, padded, LANES):
                    lane = slice(c, c + LANES)
                    v = (mine[at, group, lane] + from_peer[at, group, lane]) + (
                        ring[at_of(1, half, k), group, lane] + ring[at_of(2, half, k), group, lane])
                    mine[at, group, lane] = v
                    if c + LANES > real:
                        v = jnp.where(lax.broadcasted_iota(jnp.int32, v.shape, 1) < real - c, v, -jnp.inf)
                    tiles.append(v)
                best = top[group, :]
                old = best
                for v in tiles:
                    best = jnp.maximum(best, v)
                total = acc[group, :] * jnp.exp(old - best)
                for v in tiles:
                    total = total + jnp.exp(v - best)
                top[group, :] = best
                acc[group, :] = total
        for half in range(2):
            z_copy(half, k, last).start()

    each_chunk(finish_chunk)

    tops = jnp.concatenate([top[...], top[...]], axis=0).T
    sums = jnp.concatenate([acc[...], acc[...]], axis=0).T
    best = jnp.max(tops, axis=0, keepdims=True)
    total = jnp.sum(sums * jnp.exp(tops - best), axis=0, keepdims=True)

    def merge(items):
        new = functools.reduce(jnp.maximum, [b for b, _ in items])
        return new, functools.reduce(jnp.add, [t * jnp.exp(b - new) for b, t in items])

    stat_src[2, 0:1, :] = best
    stat_src[2, 1:2, :] = total
    for j in range(1, tp_size):
        stat_copy(2, j).start()
    items = [(best, total)]
    for j in range(1, tp_size):
        stat_copy(2, j).wait()
        items.append((stat_in[2, j - 1, 0:1, :], stat_in[2, j - 1, 1:2, :]))
    best, total = merge(items)
    v_src[0:1, :] = best
    v_src[1:2, :] = total
    for j in range(1, vp_size):
        vp_copy(v_src, v_in, v_send, v_recv, j).start()
    items = [(best, total)]
    for j in range(1, vp_size):
        vp_copy(v_src, v_in, v_send, v_recv, j).wait()
        items.append((v_in[j - 1, 0:1, :], v_in[j - 1, 1:2, :]))
    best, total = merge(items)
    ls_out[...] = jnp.broadcast_to(best + jnp.log(total), ls_out.shape)

    def drain(k, last):
        for half in range(2):
            z_copy(half, k, last).wait()
            peer_copy(3, half, k, last).wait_send()
            for phase in range(3):
                ring_copy(phase, half, k, last).wait_send()

    each_chunk(drain)


def _subtract_kernel(z, ls, nin, logprobs, log_sum, next_in):
    rows = logprobs.shape[0]
    cols = _as_columns(ls[0:1, :])[:rows]
    n = logprobs.shape[1]
    for c in range(0, n, LANES):
        w = min(LANES, n - c)
        logprobs[:, c : c + w] = z[:, c : c + w] - cols[:, :w]
    log_sum[...] = ls[0:1, :rows]
    next_in[...] = nin[...]


def solution(mesh):
    tp_size = mesh.shape["tp"]
    vp_size = mesh.shape["vp"]

    def per_device(hidden, lnf_gain, lnf_bias, emb_table, next_tok, eln_gain, eln_bias):
        rows, width = hidden.shape
        own_cols = emb_table.shape[0] // tp_size
        n_chunks = pl.cdiv(own_cols, CHUNK)
        padded = pl.cdiv(own_cols, LANES) * LANES
        f32 = jnp.float32
        vmem = pl.BlockSpec(memory_space=pltpu.VMEM)
        dma = pltpu.SemaphoreType.DMA
        z, ls, nin = pl.pallas_call(
            functools.partial(_head_kernel, tp_size, vp_size),
            out_shape=(
                jax.ShapeDtypeStruct((rows, padded), f32),
                jax.ShapeDtypeStruct((8, LANES), f32),
                jax.ShapeDtypeStruct((rows, width), jnp.bfloat16),
            ),
            in_specs=[vmem] * 6 + [pl.BlockSpec(memory_space=pl.ANY)],
            out_specs=(pl.BlockSpec(memory_space=pl.ANY), vmem, vmem),
            scratch_shapes=[
                pltpu.VMEM(emb_table.shape, emb_table.dtype),
                pltpu.VMEM((4 * n_chunks, rows, CHUNK), f32),
                pltpu.VMEM((4 * n_chunks, rows, CHUNK), f32),
                pltpu.VMEM((n_chunks, rows, CHUNK), f32),
                pltpu.VMEM((3 * n_chunks, rows, CHUNK), f32),
                pltpu.VMEM((rows, width), jnp.bfloat16),
                pltpu.VMEM((rows, LANES), f32),
                pltpu.VMEM((rows, LANES), f32),
                pltpu.VMEM((rows, width), f32),
                pltpu.VMEM((vp_size - 1, rows, width), f32),
                pltpu.VMEM((3, 8, LANES), f32),
                pltpu.VMEM((3, tp_size - 1, 8, LANES), f32),
                pltpu.VMEM((8, LANES), f32),
                pltpu.VMEM((vp_size - 1, 8, LANES), f32),
                dma((16,)),
                dma((n_chunks,)),
                dma((4 * n_chunks,)),
                dma((3 * n_chunks,)),
                dma((3 * n_chunks,)),
                dma((3, tp_size - 1)),
                dma((3, tp_size - 1)),
                dma((vp_size - 1,)),
                dma((vp_size - 1,)),
                dma((vp_size - 1,)),
                dma((vp_size - 1,)),
                dma((n_chunks,)),
            ],
            compiler_params=pltpu.CompilerParams(
                collective_id=0, has_side_effects=True, vmem_limit_bytes=63_000_000),
            name="vocab_head",
        )(
            hidden, lnf_gain.reshape(1, width), lnf_bias.reshape(1, width),
            eln_gain.reshape(1, width), eln_bias.reshape(1, width), next_tok.reshape(1, rows), emb_table,
        )
        logprobs, log_sum, next_in = pl.pallas_call(
            _subtract_kernel,
            out_shape=(
                jax.ShapeDtypeStruct((rows, own_cols), f32),
                jax.ShapeDtypeStruct((1, rows), f32),
                jax.ShapeDtypeStruct((rows, width), jnp.bfloat16),
            ),
            in_specs=[vmem] * 3,
            out_specs=(vmem,) * 3,
            name="log_probs",
        )(z, ls, nin)
        return logprobs, log_sum.reshape(rows), next_in

    return jax.shard_map(
        per_device,
        mesh=mesh,
        in_specs=(P("dp", "tp"), P("tp"), P("tp"), P("vp", "tp"), P("dp"), P("tp"), P("tp")),
        out_specs=(P("dp", ("vp", "tp")), P("dp"), P("dp", "tp")),
        check_vma=False,
    )
```

time: 355 us -> 93.6 us (0.26)
  waiting for transfers between devices: 195 us -> 0 us
  blocking collectives: 104 us -> 0 us
  Pallas kernels: 0 us -> 92.7 us
  matrix products: 25.5 us -> 0 us
  between operations: 14.1 us -> 0.64 us
  other arithmetic: 9.1 us -> 0 us
  local copies, waits for them, and re-layouts: 6.89 us -> 0 us
    unnamed x3 -> x0, waiting for transfers between devices: 158 us -> none
    pallas_call x0 -> x2, Pallas kernels: none -> 92.7 us  [the longest x1 89.7 us: per_device(): pl.pallas_call(functools.partial(_head_kernel, tp_size, vp_size), out_sha...]
    psum x2 -> x0, blocking collectives: 58.2 us -> none  [the longest x1 43.7 us: global_lse(): lax.psum(jnp.sum(jnp.exp(logits - row_top[:, None]), axis=1), ('vp', 'tp'))]
    pmax x1 -> x0, blocking collectives: 45.8 us -> none  [global_lse(): row_top = lax.pmax(jnp.max(logits, axis=1), ('vp', 'tp'))]
    psum x1 -> x0, waiting for transfers between devices: 36.6 us -> none  [per_device(): tok_rows = lax.psum(picked, 'vp')]
    unnamed x1 -> x0, matrix products: 25.5 us -> none
  transfers between devices with their start and end apart: 2 -> 0, of which waited for: 2 -> 0; matrix products, arithmetic and copies ran while one was open for 0% -> 0% of each run, Pallas kernels for 0% -> 0%
where the time goes in v1:
time: 93.6 us; the launch traced here: 93.4 us
  Pallas kernels  92.7 us (99%)
    pallas_call x1, Pallas kernels, per_device(): pl.pallas_call(functools.partial(_head_kernel, tp_size, vp_size), out_sha...  89.7 us
    pallas_call x1, Pallas kernels, per_device(): pl.pallas_call(_subtract_kernel, out_shape=(jax.ShapeDtypeStruct((rows, o...  3.07 us

profile of v1, /device:TPU:97, one launch (start us, length us, event | category | flops | bytes accessed | tf_op | source)
XLA Modules:
  0.0 93.4 jit_solution(15682700655746509048)
XLA Ops:
  0.6 89.7 %vocab_head.1 = (f32[64,7936]{1,0:T(8,128)}, f32[8,128]{1,0:T(8,128)}, bf16[64,256]{1,0:T(8,128)(2,1)}) custom-call(bf16[64,256]{1,0:T(8,128)(2,1)} %hid.1, f32[1,256]{1,0:T(1,128)} %bitcast.6, f32[1,256]{1,0:T(1,128)} %bitcast.7, f32[1,256]{1,0:T(1,128)} %bitcast.8, f32[1,256]{1,0:T(1,128)} %bitcast.9, s32[1,64]{1,0:T(1,128)} %bitcast.10, ...), custom_call_target="tpu_custom_call" | custom-call | tf_op jit(solution)/shard_map/vocab_head/pallas_call | solution.py:367
  90.3 3.1 %log_probs.1 = (f32[64,7840]{1,0:T(8,128)}, f32[1,64]{1,0:T(1,128)}, bf16[64,256]{1,0:T(8,128)(2,1)}) custom-call(f32[64,7936]{1,0:T(8,128)} %get-tuple-element.9.z, f32[8,128]{1,0:T(8,128)} %get-tuple-element.10.ls, bf16[64,256]{1,0:T(8,128)(2,1)} %get-tuple-element.11.nin), custom_call_target="tpu_custom_call" | custom-call | tf_op jit(solution)/shard_map/log_probs/pallas_call | solution.py:411

commit v2 on v1

v2 whole, which is shorter than its diff:
```python
import functools

import jax
import jax.numpy as jnp
from jax import lax
from jax.experimental import pallas as pl
from jax.experimental.pallas import tpu as pltpu
from jax.sharding import PartitionSpec as P

NORM_EPS = 1e-5
LANES = 128
CHUNK = 1024
HEAD = 256
DOT_COLS = 512
PICK = 1280
MESH_ID = pl.DeviceIdType.MESH


def _row_stats(x):
    sums = x[:, :LANES]
    squares = sums * sums
    for c in range(LANES, x.shape[1], LANES):
        part = x[:, c : c + LANES]
        sums = sums + part
        squares = squares + part * part
    both = jnp.concatenate([sums, squares], axis=0)
    return jnp.sum(both.T, axis=0, keepdims=True)


def _as_columns(row):
    return jnp.broadcast_to(row, (LANES, LANES)).T


def _normalize(x, total, gain, bias, full_width):
    rows = x.shape[0]
    cols = _as_columns(total)
    mean = cols[:rows] / full_width
    var = cols[rows : 2 * rows] / full_width - mean * mean
    rstd = lax.rsqrt(var + NORM_EPS)
    parts = []
    for c in range(0, x.shape[1], LANES):
        scaled = (x[:, c : c + LANES] - mean) * rstd
        parts.append(scaled * gain[:, c : c + LANES] + bias[:, c : c + LANES])
    return jnp.concatenate(parts, axis=1).astype(jnp.bfloat16)


def _unpacked(packed, first_row, rows_per_group, cols):
    group, r = first_row // rows_per_group, first_row % rows_per_group
    v = packed[r : r + 8, :]
    return pltpu.roll(v, LANES - group * cols, 1) if group else v


def _head_kernel(
    tp_size, vp_size,
    hid_hbm, g1_hbm, b1_hbm, g2_hbm, b2_hbm, tok_hbm, emb,
    z_out, ls_out, nin_out,
    hid, norms, tok,
    e_all, mine, from_peer, to_peer, ring, xn,
    top, acc, e_src, e_in, stat_src, stat_in, lse_src, lse_tp, lse_vp,
    small_sem, e_sem, peer_send, peer_recv, ring_send, ring_recv, head_send, head_recv,
    stat_send, stat_recv, row_sem, lse_sem,
):
    rows, width = hid.shape
    full_width = width * tp_size
    vocab_rows = emb.shape[0]
    own_cols = vocab_rows // tp_size
    chips = tp_size // 2
    n_chunks = pl.cdiv(own_cols, CHUNK)
    half_chunks = n_chunks // 2
    half_cols = half_chunks * CHUNK
    tail = own_cols - (n_chunks - 1) * CHUNK
    rest = tail % LANES
    rest_rows = rows * rest // LANES

    def buffer_rows(cols):
        return cols // LANES * rows + (rest_rows if cols % LANES else 0)

    me = lax.axis_index("tp")
    my_vp = lax.axis_index("vp")
    chip = me // 2
    core = me % 2
    peer = 2 * chip + 1 - core
    turn = 1 - 2 * core

    def chip_at(offset):
        return (chip + offset + chips) % chips

    fwd = 2 * chip_at(turn) + core
    bwd = 2 * chip_at(-turn) + core

    barrier = pltpu.get_barrier_semaphore()
    far_first = sorted(range(1, tp_size), key=lambda j: -min(j, tp_size - j))
    for j in far_first:
        pl.semaphore_signal(barrier, inc=1, device_id={"tp": (me + j) % tp_size}, device_id_type=MESH_ID)
    for j in range(1, vp_size):
        pl.semaphore_signal(barrier, inc=1, device_id={"vp": (my_vp + j) % vp_size}, device_id_type=MESH_ID)

    hid_load = pltpu.make_async_copy(hid_hbm, hid, small_sem.at[0])
    tok_load = pltpu.make_async_copy(tok_hbm, tok, small_sem.at[1])
    hid_load.start()
    for i, src in enumerate([g1_hbm, b1_hbm, g2_hbm, b2_hbm]):
        pltpu.make_async_copy(src, norms.at[i], small_sem.at[2]).start()
    tok_load.start()

    def block_of(phase, half, sign):
        if phase == 0:
            return chip_at(2)
        if phase == 3:
            return chip
        if (phase == 1) == (half == 0):
            return chip_at(-sign)
        return chip_at(sign)

    def first_row(phase, half, own):
        if own:
            return (2 * block_of(phase, half, turn) + core) * own_cols + half * half_cols
        return (2 * block_of(phase, half, -turn) + 1 - core) * own_cols + half * half_cols

    def table_load(phase, half, own):
        count = half_cols if half == 0 else own_cols - half_cols
        span = pl.ds(pl.multiple_of(first_row(phase, half, own), 16), count)
        return pltpu.make_async_copy(emb.at[span], e_all.at[span], e_sem.at[phase])

    def wait_table(phase):
        span = pl.ds(0, 2 * own_cols)
        pltpu.make_async_copy(emb.at[span], e_all.at[span], e_sem.at[phase]).wait()

    hid_load.wait()
    pltpu.make_async_copy(norms, norms, small_sem.at[2]).wait()
    tok_load.wait()
    for phase in range(4):
        for own in range(2):
            for half in range(2):
                table_load(phase, half, own).start()

    def share(src, dst, send, recv, axis, j):
        size, at = (tp_size, me) if axis == "tp" else (vp_size, my_vp)
        return pltpu.make_async_remote_copy(
            src_ref=src, dst_ref=dst.at[j - 1], send_sem=send, recv_sem=recv,
            device_id={axis: (at + j) % size}, device_id_type=MESH_ID)

    def all_shared(dst, send, recv, axis):
        at = (me + 1) % tp_size if axis == "tp" else (my_vp + 1) % vp_size
        return pltpu.make_async_remote_copy(
            src_ref=dst, dst_ref=dst, send_sem=send, recv_sem=recv,
            device_id={axis: at}, device_id_type=MESH_ID)

    def share_stats(s):
        for j in far_first:
            share(stat_src.at[s], stat_in.at[s], stat_send.at[s], stat_recv.at[s], "tp", j).start()

    def stat_total(s):
        all_shared(stat_in.at[s], stat_send.at[s], stat_recv.at[s], "tp").wait_recv()
        total = stat_src[s]
        for j in range(1, tp_size):
            total = total + stat_in[s, j - 1]
        return total

    x = hid[...].astype(jnp.float32)
    stat_src[0] = _row_stats(x)
    pl.semaphore_wait(barrier, tp_size - 1 + vp_size - 1)
    share_stats(0)
    xn[...] = _normalize(x, stat_total(0), norms[0], norms[1], full_width)

    def chunk_dot(dst, base, row0, first, cols):
        for c in range(first, cols, DOT_COLS):
            n = min(DOT_COLS, cols - c)
            part = e_all[pl.ds(pl.multiple_of(row0 + c, 16), n), :]
            v = lax.dot_general(xn[...], part, (((1,), (1,)), ((), ())), preferred_element_type=jnp.float32)
            for t in range(0, n, LANES):
                at = base + (c + t) // LANES * rows
                if t + LANES <= n:
                    dst[pl.ds(at, rows), :] = v[:, t : t + LANES]
                else:
                    dst[pl.ds(at, rest_rows), :] = jnp.concatenate(
                        [v[q : q + rest_rows, t:n] for q in range(0, rows, rest_rows)], axis=1)

    def cols_of(half, last):
        return tail if half == 1 and last else CHUNK

    def at_of(phase, half, k):
        return phase * n_chunks + half * half_chunks + k

    own_rows = buffer_rows(own_cols)

    def base_of(phase, half, k):
        return pl.multiple_of(phase * own_rows + (half * half_chunks + k) * buffer_rows(CHUNK), 8)

    def span_of(phase, half, k, last):
        begin = buffer_rows(HEAD) if phase == 0 and isinstance(k, int) and k == 0 else 0
        return pl.ds(base_of(phase, half, k) + begin, buffer_rows(cols_of(half, last)) - begin)

    def peer_sems(phase, half, k):
        slot = half * half_chunks + k
        return peer_send.at[slot], peer_recv.at[phase * n_chunks + slot if phase < 2 else 2 * n_chunks + phase - 2]

    def peer_copy(phase, half, k, last):
        into = span_of(phase, half, k, last)
        begin = into.start - base_of(phase, half, k)
        slot = half * half_chunks + k
        send, recv = peer_sems(phase, half, k)
        return pltpu.make_async_remote_copy(
            src_ref=to_peer.at[slot, pl.ds(begin, into.size)], dst_ref=from_peer.at[into],
            send_sem=send, recv_sem=recv, device_id={"tp": peer}, device_id_type=MESH_ID)

    def ring_recv_of(phase, half, k):
        return ring_recv.at[phase if phase < 2 else 2 + half * half_chunks + k]

    def ring_copy(phase, half, k, last):
        span = span_of(phase, half, k, last)
        forward = (half == 0) != (phase == 1)
        return pltpu.make_async_remote_copy(
            src_ref=mine.at[span], dst_ref=ring.at[span],
            send_sem=ring_send.at[0], recv_sem=ring_recv_of(phase, half, k),
            device_id={"tp": fwd if forward else bwd}, device_id_type=MESH_ID)

    def whole_phase(ref, phase):
        return ref.at[pl.ds(phase * own_rows, own_rows)]

    def wait_peer_phase(phase):
        ref = whole_phase(from_peer, phase)
        pltpu.make_async_remote_copy(
            src_ref=ref, dst_ref=ref, send_sem=peer_send.at[0], recv_sem=peer_sems(phase, 0, 0)[1],
            device_id={"tp": peer}, device_id_type=MESH_ID).wait_recv()

    def wait_ring_phase(phase):
        ref = whole_phase(ring, phase)
        pltpu.make_async_remote_copy(
            src_ref=ref, dst_ref=ref, send_sem=ring_send.at[0], recv_sem=ring_recv.at[phase],
            device_id={"tp": fwd}, device_id_type=MESH_ID).wait_recv()

    head_rows = pl.ds(0, buffer_rows(HEAD))

    def head_peer_copy(half):
        slot = half * half_chunks
        return pltpu.make_async_remote_copy(
            src_ref=to_peer.at[slot, head_rows], dst_ref=from_peer.at[pl.ds(slot * buffer_rows(CHUNK), head_rows.size)],
            send_sem=head_send.at[half], recv_sem=head_recv.at[half],
            device_id={"tp": peer}, device_id_type=MESH_ID)

    def head_ring_copy(half):
        span = pl.ds(half * half_chunks * buffer_rows(CHUNK), head_rows.size)
        return pltpu.make_async_remote_copy(
            src_ref=mine.at[span], dst_ref=ring.at[span],
            send_sem=ring_send.at[0], recv_sem=ring_recv.at[0],
            device_id={"tp": bwd if half else fwd}, device_id_type=MESH_ID)

    def add_into(base, others, begin, end):
        for r in range(begin, end, 8):
            v = mine[pl.ds(base + r, 8), :]
            for ref, at in others:
                v = v + ref[pl.ds(at + r, 8), :]
            mine[pl.ds(base + r, 8), :] = v

    def to_peer_dot(phase, half, k, last, first=0, end=None):
        chunk_dot(to_peer.at[half * half_chunks + k], 0, first_row(phase, half, 0) + k * CHUNK,
                  first, end or cols_of(half, last))

    def mine_dot(phase, half, k, last, first=0, end=None):
        if phase < 3:
            dst, base = mine, base_of(phase, half, k)
        else:
            dst, base = z_out, base_of(0, half, k)
        chunk_dot(dst, base, first_row(phase, half, 1) + k * CHUNK, first, end or cols_of(half, last))

    def first_product():
        for half in range(2):
            to_peer_dot(0, half, 0, False, 0, HEAD)
        for half in range(2):
            head_peer_copy(half).start()
        for half in range(2):
            mine_dot(0, half, 0, False, 0, HEAD)
        for half in range(2):
            to_peer_dot(0, half, 0, False, HEAD)
        for half in range(2):
            peer_copy(0, half, 0, False).start()
        for half in range(2):
            at = base_of(0, half, 0)
            head_peer_copy(half).wait_recv()
            add_into(at, [(from_peer, at)], 0, buffer_rows(HEAD))
        for half in range(2):
            head_ring_copy(half).start()
        for half in range(2):
            mine_dot(0, half, 0, False, HEAD)
        for half in range(2):
            at = base_of(0, half, 0)
            peer_copy(0, half, 0, False).wait_recv()
            add_into(at, [(from_peer, at)], buffer_rows(HEAD), buffer_rows(CHUNK))
        for half in range(2):
            ring_copy(0, half, 0, False).start()
        for half in range(2):
            head_peer_copy(half).wait_send()

    def product(phase, k, last):
        for half in range(2):
            if phase:
                peer_copy(phase - 1, half, k, last).wait_send()
            to_peer_dot(phase, half, k, last)
        for half in range(2):
            peer_copy(phase, half, k, last).start()
        for half in range(2):
            mine_dot(phase, half, k, last)
        if phase < 2:
            for half in range(2):
                at = base_of(phase, half, k)
                peer_copy(phase, half, k, last).wait_recv()
                add_into(at, [(from_peer, at)], 0, buffer_rows(cols_of(half, last)))
            for half in range(2):
                ring_copy(phase, half, k, last).start()

    def each_chunk(body, begin=0):
        def step(k, carry):
            body(k, False)
            return carry

        for k in range(begin, 1):
            body(k, False)
        lax.fori_loop(1, half_chunks - 1, step, 0)
        body(half_chunks - 1, True)

    wait_table(0)
    first_product()
    each_chunk(functools.partial(product, 0), 1)

    for phase in range(1, 4):
        wait_table(phase)

    def pick_rows():
        wanted = tok[...].astype(jnp.float32) - (my_vp * vocab_rows).astype(jnp.float32)
        wanted = jnp.concatenate([wanted, jnp.zeros((1, LANES - rows), jnp.float32)], axis=1)
        wanted = _as_columns(wanted)[:rows].astype(jnp.int32)
        lane = lax.broadcasted_iota(jnp.int32, wanted.shape, 1)

        def add(first, count):
            hits = []
            for c in range(0, count, LANES):
                hits.append(jnp.where(lane + (first + c) == wanted, 1.0, 0.0).astype(jnp.bfloat16))
            e_src[...] += jnp.dot(
                jnp.concatenate(hits, axis=1), e_all[pl.ds(pl.multiple_of(first, LANES), count), :],
                preferred_element_type=jnp.float32)

        def step(i, carry):
            add(i * PICK, PICK)
            return carry

        e_src[...] = jnp.zeros_like(e_src)
        lax.fori_loop(0, vocab_rows // PICK, step, 0)
        if vocab_rows % PICK:
            add(vocab_rows // PICK * PICK, vocab_rows % PICK)

    each_chunk(functools.partial(product, 1))
    pick_rows()
    for j in range(1, vp_size):
        share(e_src, e_in, row_sem.at[0], row_sem.at[1], "vp", j).start()
    each_chunk(functools.partial(product, 2))

    def token_rows():
        rows_sum = e_src[...]
        for j in range(1, vp_size):
            rows_sum = rows_sum + e_in[j - 1]
        return rows_sum

    all_shared(e_in, row_sem.at[0], row_sem.at[1], "vp").wait()
    stat_src[1] = _row_stats(token_rows())
    share_stats(1)

    def forward_chunk(k, last):
        for half in range(2):
            at = base_of(2, half, k)
            add_into(at, [(from_peer, at), (ring, base_of(0, half, k))], 0, buffer_rows(cols_of(half, last)))
        for half in range(2):
            ring_copy(2, half, k, last).start()

    wait_peer_phase(2)
    wait_ring_phase(0)
    each_chunk(forward_chunk)
    each_chunk(functools.partial(product, 3))
    nin_out[...] = _normalize(token_rows(), stat_total(1), norms[2], norms[3], full_width)

    top[...] = jnp.full(top.shape, jnp.finfo(jnp.float32).min, jnp.float32)
    acc[...] = jnp.zeros_like(acc)

    def finish_chunk(k, last):
        for half in range(2):
            cols = cols_of(half, last)
            base, peer_base = base_of(0, half, k), base_of(3, half, k)
            single, chain = base_of(1, half, k), base_of(2, half, k)
            ring_copy(2, half, k, last).wait_recv()

            def final(r):
                v = (z_out[pl.ds(base + r, 8), :] + from_peer[pl.ds(peer_base + r, 8), :]) + (
                    ring[pl.ds(single + r, 8), :] + ring[pl.ds(chain + r, 8), :])
                z_out[pl.ds(base + r, 8), :] = v
                return v

            full = cols // LANES
            if cols % LANES:
                packed = jnp.concatenate([final(full * rows + r) for r in range(0, rest_rows, 8)], axis=0)
            for r in range(0, rows, 8):
                tiles = [final(t * rows + r) for t in range(full)]
                if cols % LANES:
                    v = _unpacked(packed, r, rest_rows, rest)
                    tiles.append(jnp.where(lax.broadcasted_iota(jnp.int32, v.shape, 1) < rest, v, -jnp.inf))
                old = top[r : r + 8, :]
                best = functools.reduce(jnp.maximum, tiles, old)
                total = acc[r : r + 8, :] * jnp.exp(old - best)
                for v in tiles:
                    total = total + jnp.exp(v - best)
                top[r : r + 8, :] = best
                acc[r : r + 8, :] = total

    wait_peer_phase(3)
    wait_ring_phase(1)
    each_chunk(finish_chunk)

    tops = jnp.concatenate([top[...], top[...]], axis=0).T
    sums = jnp.concatenate([acc[...], acc[...]], axis=0).T
    best = jnp.max(tops, axis=0, keepdims=True)
    total = jnp.sum(sums * jnp.exp(tops - best), axis=0, keepdims=True)

    def merge(best, total, other):
        tops = [best] + [other[j, 0:1, :] for j in range(other.shape[0])]
        sums = [total] + [other[j, 1:2, :] for j in range(other.shape[0])]
        new = functools.reduce(jnp.maximum, tops)
        return new, functools.reduce(jnp.add, [t * jnp.exp(b - new) for b, t in zip(tops, sums)])

    stages = (("tp", far_first, lse_tp), ("vp", range(1, vp_size), lse_vp))
    for i, (axis, order, other) in enumerate(stages):
        lse_src[i, 0:1, :] = best
        lse_src[i, 1:2, :] = total
        for j in order:
            share(lse_src.at[i], other, lse_sem.at[2 * i], lse_sem.at[2 * i + 1], axis, j).start()
        all_shared(other, lse_sem.at[2 * i], lse_sem.at[2 * i + 1], axis).wait_recv()
        best, total = merge(best, total, other)
    ls_out[...] = jnp.broadcast_to(best + jnp.log(total), ls_out.shape)

    for s in range(2):
        all_shared(stat_in.at[s], stat_send.at[s], stat_recv.at[s], "tp").wait_send()
    for i, (axis, _, other) in enumerate(stages):
        all_shared(other, lse_sem.at[2 * i], lse_sem.at[2 * i + 1], axis).wait_send()
    pltpu.make_async_remote_copy(
        src_ref=mine, dst_ref=ring, send_sem=ring_send.at[0], recv_sem=ring_recv.at[0],
        device_id={"tp": fwd}, device_id_type=MESH_ID).wait_send()
    each_chunk(lambda k, last: [peer_copy(3, half, k, last).wait_send() for half in range(2)])


def _subtract_kernel(z, ls, nin, logprobs, log_sum, next_in, out, sums, sems):
    rows, n = out.shape
    rest = n % LANES
    rest_rows = rows * rest // LANES
    step = rows // 4
    copies = [
        pltpu.make_async_copy(nin, next_in, sems.at[4]),
        pltpu.make_async_copy(sums, log_sum, sems.at[5]),
    ]
    copies[0].start()
    sums[...] = ls[0:1, :rows]
    cols = _as_columns(ls[0:1, :])[:rows]
    packed = z[n // LANES * rows :, :]
    for i in range(4):
        for r in range(i * step, (i + 1) * step, 8):
            for t in range(n // LANES):
                out[r : r + 8, t * LANES : (t + 1) * LANES] = z[t * rows + r : t * rows + r + 8, :] - cols[r : r + 8]
            if rest:
                v = _unpacked(packed, r, rest_rows, rest) - cols[r : r + 8]
                out[r : r + 8, n - rest :] = v[:, :rest]
        span = pl.ds(i * step, step)
        copies.append(pltpu.make_async_copy(out.at[span], logprobs.at[span], sems.at[i]))
        copies[-1].start()
        if i == 0:
            copies[1].start()
    for copy in copies:
        copy.wait()


def solution(mesh):
    tp_size = mesh.shape["tp"]
    vp_size = mesh.shape["vp"]

    def per_device(hidden, lnf_gain, lnf_bias, emb_table, next_tok, eln_gain, eln_bias):
        rows, width = hidden.shape
        own_cols = emb_table.shape[0] // tp_size
        n_chunks = pl.cdiv(own_cols, CHUNK)
        f32 = jnp.float32
        vmem = pl.BlockSpec(memory_space=pltpu.VMEM)
        hbm = pl.BlockSpec(memory_space=pltpu.HBM)
        dma = pltpu.SemaphoreType.DMA
        own_rows = rows * own_cols // LANES
        z, ls, nin = pl.pallas_call(
            functools.partial(_head_kernel, tp_size, vp_size),
            out_shape=(
                pltpu.VMEM((own_rows, LANES), f32),
                pltpu.VMEM((8, LANES), f32),
                pltpu.VMEM((rows, width), jnp.bfloat16),
            ),
            in_specs=[hbm] * 7,
            out_specs=(vmem,) * 3,
            scratch_shapes=[
                pltpu.VMEM((rows, width), hidden.dtype),
                pltpu.VMEM((4, 1, width), f32),
                pltpu.VMEM((1, rows), jnp.int32),
                pltpu.VMEM(emb_table.shape, emb_table.dtype),
                pltpu.VMEM((3 * own_rows, LANES), f32),
                pltpu.VMEM((4 * own_rows, LANES), f32),
                pltpu.VMEM((n_chunks, rows * CHUNK // LANES, LANES), f32),
                pltpu.VMEM((3 * own_rows, LANES), f32),
                pltpu.VMEM((rows, width), jnp.bfloat16),
                pltpu.VMEM((rows, LANES), f32),
                pltpu.VMEM((rows, LANES), f32),
                pltpu.VMEM((rows, width), f32),
                pltpu.VMEM((vp_size - 1, rows, width), f32),
                pltpu.VMEM((2, 1, LANES), f32),
                pltpu.VMEM((2, tp_size - 1, 1, LANES), f32),
                pltpu.VMEM((2, 2, LANES), f32),
                pltpu.VMEM((tp_size - 1, 2, LANES), f32),
                pltpu.VMEM((vp_size - 1, 2, LANES), f32),
                dma((3,)),
                dma((4,)),
                dma((n_chunks,)),
                dma((2 * n_chunks + 2,)),
                dma((1,)),
                dma((2 + n_chunks,)),
                dma((2,)),
                dma((2,)),
                dma((2,)),
                dma((2,)),
                dma((2,)),
                dma((4,)),
            ],
            compiler_params=pltpu.CompilerParams(
                collective_id=0, has_side_effects=True, vmem_limit_bytes=58_000_000),
            name="vocab_head",
        )(
            hidden, lnf_gain.reshape(1, width), lnf_bias.reshape(1, width),
            eln_gain.reshape(1, width), eln_bias.reshape(1, width), next_tok.reshape(1, rows), emb_table,
        )
        logprobs, log_sum, next_in = pl.pallas_call(
            _subtract_kernel,
            out_shape=(
                jax.ShapeDtypeStruct((rows, own_cols), f32),
                jax.ShapeDtypeStruct((1, rows), f32),
                jax.ShapeDtypeStruct((rows, width), jnp.bfloat16),
            ),
            in_specs=[vmem] * 3,
            out_specs=(hbm,) * 3,
            scratch_shapes=[pltpu.VMEM((rows, own_cols), f32), pltpu.VMEM((1, rows), f32), dma((6,))],
            compiler_params=pltpu.CompilerParams(vmem_limit_bytes=16_000_000),
            name="log_probs",
        )(z, ls, nin)
        return logprobs, log_sum.reshape(rows), next_in

    return jax.shard_map(
        per_device,
        mesh=mesh,
        in_specs=(P("dp", "tp"), P("tp"), P("tp"), P("vp", "tp"), P("dp"), P("tp"), P("tp")),
        out_specs=(P("dp", ("vp", "tp")), P("dp"), P("dp", "tp")),
        check_vma=False,
    )
```

time: 93.6 us -> 87.7 us (0.937)
  Pallas kernels: 92.7 us -> 86.9 us
    pallas_call x1, Pallas kernels: 89.7 us -> 85.4 us  [per_device(): pl.pallas_call(functools.partial(_head_kernel, tp_size, vp_size), out_sha...]
    pallas_call x1, Pallas kernels: 3.07 us -> 1.47 us  [per_device(): pl.pallas_call(_subtract_kernel, out_shape=(jax.ShapeDtypeStruct((rows, o...]
where the time goes in v2:
time: 87.7 us; the launch traced here: 87.5 us
  Pallas kernels  86.9 us (99%)
    pallas_call x1, Pallas kernels, per_device(): pl.pallas_call(functools.partial(_head_kernel, tp_size, vp_size), out_sha...  85.4 us

profile of v2, /device:TPU:97, one launch (start us, length us, event | category | flops | bytes accessed | tf_op | source)
XLA Modules:
  0.0 87.5 jit_solution(10208260393702395495)
XLA Ops:
  0.6 85.4 %vocab_head.1 = (f32[3920,128]{1,0:T(8,128)S(1)}, f32[8,128]{1,0:T(8,128)S(1)}, bf16[64,256]{1,0:T(8,128)(2,1)S(1)}) custom-call(bf16[64,256]{1,0:T(8,128)(2,1)} %hid_hbm.1, f32[1,256]{1,0:T(1,128)} %bitcast.6, f32[1,256]{1,0:T(1,128)} %bitcast.7, f32[1,256]{1,0:T(1,128)} %bitcast.8, f32[1,256]{1,0:T(1,128)} %bitcast.9, s32[1,64]{1,0:T(1,128)} %bitcast.10, ...), custom_call_target="tpu_custom_call" | custom-call | tf_op jit(solution)/shard_map/vocab_head/pallas_call | solution.py:489
  86.0 1.5 %log_probs.1 = (f32[64,7840]{1,0:T(8,128)}, f32[1,64]{1,0:T(1,128)}, bf16[64,256]{1,0:T(8,128)(2,1)}) custom-call(f32[3920,128]{1,0:T(8,128)S(1)} %get-tuple-element.9.z, f32[8,128]{1,0:T(8,128)S(1)} %get-tuple-element.10.ls, bf16[64,256]{1,0:T(8,128)(2,1)S(1)} %get-tuple-element.11.nin), custom_call_target="tpu_custom_call" | custom-call | tf_op jit(solution)/shard_map/log_probs/pallas_call | solution.py:537

commit v3 on v2

--- a/solution.py
+++ b/solution.py
@@ -10,7 +10,7 @@
 NORM_EPS = 1e-5
 LANES = 128
 CHUNK = 1024
-HEAD = 256
+HEAD = 384
 DOT_COLS = 512
 PICK = 1280
 MESH_ID = pl.DeviceIdType.MESH
@@ -31,12 +31,14 @@
     return jnp.broadcast_to(row, (LANES, LANES)).T
 
 
-def _normalize(x, total, gain, bias, full_width):
-    rows = x.shape[0]
+def _mean_rstd(total, rows, full_width):
     cols = _as_columns(total)
     mean = cols[:rows] / full_width
     var = cols[rows : 2 * rows] / full_width - mean * mean
-    rstd = lax.rsqrt(var + NORM_EPS)
+    return mean, lax.rsqrt(var + NORM_EPS)
+
+
+def _normalize(x, mean, rstd, gain, bias):
     parts = []
     for c in range(0, x.shape[1], LANES):
         scaled = (x[:, c : c + LANES] - mean) * rstd
@@ -55,10 +57,10 @@
     hid_hbm, g1_hbm, b1_hbm, g2_hbm, b2_hbm, tok_hbm, emb,
     z_out, ls_out, nin_out,
     hid, norms, tok,
-    e_all, mine, from_peer, to_peer, ring, xn,
-    top, acc, e_src, e_in, stat_src, stat_in, lse_src, lse_tp, lse_vp,
-    small_sem, e_sem, peer_send, peer_recv, ring_send, ring_recv, head_send, head_recv,
-    stat_send, stat_recv, row_sem, lse_sem,
+    e_all, mine, from_peer, to_peer, ring, xn, xn_peer, early, early_out, early_in, early_rows,
+    top, acc, e_src, e_in, stat_src, stat_in, lse_src, lse_in,
+    small_sem, e_sem, early_sem, peer_send, peer_recv, ring_send, ring_recv,
+    stat_send, stat_recv, row_sem, lse_send, lse_recv,
 ):
     rows, width = hid.shape
     full_width = width * tp_size
@@ -119,11 +121,15 @@
     def table_load(phase, half, own):
         count = half_cols if half == 0 else own_cols - half_cols
         span = pl.ds(pl.multiple_of(first_row(phase, half, own), 16), count)
-        return pltpu.make_async_copy(emb.at[span], e_all.at[span], e_sem.at[phase])
-
-    def wait_table(phase):
-        span = pl.ds(0, 2 * own_cols)
-        pltpu.make_async_copy(emb.at[span], e_all.at[span], e_sem.at[phase]).wait()
+        return pltpu.make_async_copy(emb.at[span], e_all.at[span], e_sem.at[min(phase, 1)])
+
+    def wait_table(phases):
+        span = pl.ds(0, 2 * own_cols * phases)
+        pltpu.make_async_copy(emb.at[span], e_all.at[span], e_sem.at[min(phases - 1, 1)]).wait()
+
+    for half in range(2):
+        rows_at = pl.ds(pl.multiple_of(first_row(0, half, 0), 16), HEAD)
+        pltpu.make_async_copy(emb.at[rows_at], early.at[pl.ds(half * HEAD, HEAD)], early_sem.at[0]).start()
 
     hid_load.wait()
     pltpu.make_async_copy(norms, norms, small_sem.at[2]).wait()
@@ -147,10 +153,10 @@
 
     def share_stats(s):
         for j in far_first:
-            share(stat_src.at[s], stat_in.at[s], stat_send.at[s], stat_recv.at[s], "tp", j).start()
+            share(stat_src.at[s], stat_in.at[s], stat_send.at[0], stat_recv.at[s], "tp", j).start()
 
     def stat_total(s):
-        all_shared(stat_in.at[s], stat_send.at[s], stat_recv.at[s], "tp").wait_recv()
+        all_shared(stat_in.at[s], stat_send.at[0], stat_recv.at[s], "tp").wait_recv()
         total = stat_src[s]
         for j in range(1, tp_size):
             total = total + stat_in[s, j - 1]
@@ -158,9 +164,24 @@
 
     x = hid[...].astype(jnp.float32)
     stat_src[0] = _row_stats(x)
+    early_out[pl.ds(2 * HEAD, rows), :] = x
+    early_out[pl.ds(2 * HEAD + rows, 8), :] = jnp.concatenate(
+        [norms[0], norms[1], jnp.zeros((6, width), jnp.float32)], axis=0)
+    pltpu.make_async_copy(emb.at[pl.ds(0, 2 * HEAD)], early, early_sem.at[0]).wait()
+    early_out[pl.ds(0, 2 * HEAD), :] = early[...].astype(jnp.float32)
     pl.semaphore_wait(barrier, tp_size - 1 + vp_size - 1)
     share_stats(0)
-    xn[...] = _normalize(x, stat_total(0), norms[0], norms[1], full_width)
+    early_copy = pltpu.make_async_remote_copy(
+        src_ref=early_out, dst_ref=early_in, send_sem=early_sem.at[1], recv_sem=early_sem.at[2],
+        device_id={"tp": peer}, device_id_type=MESH_ID)
+    early_copy.start()
+    early_copy.wait_recv()
+    early_rows[...] = early_in[pl.ds(0, 2 * HEAD), :].astype(jnp.bfloat16)
+    mean, rstd = _mean_rstd(stat_total(0), rows, full_width)
+    xn[...] = _normalize(x, mean, rstd, norms[0], norms[1])
+    xn_peer[...] = _normalize(
+        early_in[pl.ds(2 * HEAD, rows), :], mean, rstd,
+        early_in[pl.ds(2 * HEAD + rows, 1), :], early_in[pl.ds(2 * HEAD + rows + 1, 1), :])
 
     def chunk_dot(dst, base, row0, first, cols):
         for c in range(first, cols, DOT_COLS):
@@ -190,18 +211,27 @@
         begin = buffer_rows(HEAD) if phase == 0 and isinstance(k, int) and k == 0 else 0
         return pl.ds(base_of(phase, half, k) + begin, buffer_rows(cols_of(half, last)) - begin)
 
-    def peer_sems(phase, half, k):
-        slot = half * half_chunks + k
-        return peer_send.at[slot], peer_recv.at[phase * n_chunks + slot if phase < 2 else 2 * n_chunks + phase - 2]
+    def peer_recv_of(phase, k):
+        return peer_recv.at[k if phase == 0 else half_chunks + phase - 1]
 
     def peer_copy(phase, half, k, last):
-        into = span_of(phase, half, k, last)
-        begin = into.start - base_of(phase, half, k)
-        slot = half * half_chunks + k
-        send, recv = peer_sems(phase, half, k)
+        span = span_of(phase, half, k, last)
         return pltpu.make_async_remote_copy(
-            src_ref=to_peer.at[slot, pl.ds(begin, into.size)], dst_ref=from_peer.at[into],
-            send_sem=send, recv_sem=recv, device_id={"tp": peer}, device_id_type=MESH_ID)
+            src_ref=to_peer.at[span], dst_ref=from_peer.at[span],
+            send_sem=peer_send.at[0], recv_sem=peer_recv_of(phase, k),
+            device_id={"tp": peer}, device_id_type=MESH_ID)
+
+    def wait_peer(recv, count):
+        ref = from_peer.at[pl.ds(0, count)]
+        pltpu.make_async_remote_copy(
+            src_ref=ref, dst_ref=ref, send_sem=peer_send.at[0], recv_sem=recv,
+            device_id={"tp": peer}, device_id_type=MESH_ID).wait_recv()
+
+    def wait_peer_phase(phase):
+        wait_peer(peer_recv_of(phase, 0), own_rows)
+
+    def wait_peer_chunk(k, last):
+        wait_peer(peer_recv_of(0, k), sum(span_of(0, half, k, last).size for half in range(2)))
 
     def ring_recv_of(phase, half, k):
         return ring_recv.at[phase if phase < 2 else 2 + half * half_chunks + k]
@@ -217,12 +247,6 @@
     def whole_phase(ref, phase):
         return ref.at[pl.ds(phase * own_rows, own_rows)]
 
-    def wait_peer_phase(phase):
-        ref = whole_phase(from_peer, phase)
-        pltpu.make_async_remote_copy(
-            src_ref=ref, dst_ref=ref, send_sem=peer_send.at[0], recv_sem=peer_sems(phase, 0, 0)[1],
-            device_id={"tp": peer}, device_id_type=MESH_ID).wait_recv()
-
     def wait_ring_phase(phase):
         ref = whole_phase(ring, phase)
         pltpu.make_async_remote_copy(
@@ -230,13 +254,6 @@
             device_id={"tp": fwd}, device_id_type=MESH_ID).wait_recv()
 
     head_rows = pl.ds(0, buffer_rows(HEAD))
-
-    def head_peer_copy(half):
-        slot = half * half_chunks
-        return pltpu.make_async_remote_copy(
-            src_ref=to_peer.at[slot, head_rows], dst_ref=from_peer.at[pl.ds(slot * buffer_rows(CHUNK), head_rows.size)],
-            send_sem=head_send.at[half], recv_sem=head_recv.at[half],
-            device_id={"tp": peer}, device_id_type=MESH_ID)
 
     def head_ring_copy(half):
         span = pl.ds(half * half_chunks * buffer_rows(CHUNK), head_rows.size)
@@ -253,7 +270,7 @@
             mine[pl.ds(base + r, 8), :] = v
 
     def to_peer_dot(phase, half, k, last, first=0, end=None):
-        chunk_dot(to_peer.at[half * half_chunks + k], 0, first_row(phase, half, 0) + k * CHUNK,
+        chunk_dot(to_peer, base_of(phase, half, k), first_row(phase, half, 0) + k * CHUNK,
                   first, end or cols_of(half, last))
 
     def mine_dot(phase, half, k, last, first=0, end=None):
@@ -265,48 +282,44 @@
 
     def first_product():
         for half in range(2):
-            to_peer_dot(0, half, 0, False, 0, HEAD)
-        for half in range(2):
-            head_peer_copy(half).start()
-        for half in range(2):
-            mine_dot(0, half, 0, False, 0, HEAD)
+            part = e_all[pl.ds(pl.multiple_of(first_row(0, half, 1), 16), HEAD), :]
+            dims = (((1,), (1,)), ((), ()))
+            v = lax.dot_general(xn[...], part, dims, preferred_element_type=jnp.float32) + lax.dot_general(
+                xn_peer[...], early_rows[pl.ds(half * HEAD, HEAD), :], dims, preferred_element_type=jnp.float32)
+            for t in range(0, HEAD, LANES):
+                mine[pl.ds(base_of(0, half, 0) + t // LANES * rows, rows), :] = v[:, t : t + LANES]
+        for half in range(2):
+            head_ring_copy(half).start()
         for half in range(2):
             to_peer_dot(0, half, 0, False, HEAD)
         for half in range(2):
             peer_copy(0, half, 0, False).start()
         for half in range(2):
+            mine_dot(0, half, 0, False, HEAD)
+        wait_peer_chunk(0, False)
+        for half in range(2):
             at = base_of(0, half, 0)
-            head_peer_copy(half).wait_recv()
-            add_into(at, [(from_peer, at)], 0, buffer_rows(HEAD))
-        for half in range(2):
-            head_ring_copy(half).start()
-        for half in range(2):
-            mine_dot(0, half, 0, False, HEAD)
-        for half in range(2):
-            at = base_of(0, half, 0)
-            peer_copy(0, half, 0, False).wait_recv()
             add_into(at, [(from_peer, at)], buffer_rows(HEAD), buffer_rows(CHUNK))
         for half in range(2):
             ring_copy(0, half, 0, False).start()
-        for half in range(2):
-            head_peer_copy(half).wait_send()
+
+    def join(phase, k, last):
+        for half in range(2):
+            at = base_of(phase, half, k)
+            add_into(at, [(from_peer, at)], 0, buffer_rows(cols_of(half, last)))
+        for half in range(2):
+            ring_copy(phase, half, k, last).start()
 
     def product(phase, k, last):
         for half in range(2):
-            if phase:
-                peer_copy(phase - 1, half, k, last).wait_send()
             to_peer_dot(phase, half, k, last)
         for half in range(2):
             peer_copy(phase, half, k, last).start()
         for half in range(2):
             mine_dot(phase, half, k, last)
-        if phase < 2:
-            for half in range(2):
-                at = base_of(phase, half, k)
-                peer_copy(phase, half, k, last).wait_recv()
-                add_into(at, [(from_peer, at)], 0, buffer_rows(cols_of(half, last)))
-            for half in range(2):
-                ring_copy(phase, half, k, last).start()
+        if phase == 0:
+            wait_peer_chunk(k, last)
+            join(phase, k, last)
 
     def each_chunk(body, begin=0):
         def step(k, carry):
@@ -318,12 +331,11 @@
         lax.fori_loop(1, half_chunks - 1, step, 0)
         body(half_chunks - 1, True)
 
-    wait_table(0)
+    wait_table(1)
     first_product()
     each_chunk(functools.partial(product, 0), 1)
 
-    for phase in range(1, 4):
-        wait_table(phase)
+    wait_table(3)
 
     def pick_rows():
         wanted = tok[...].astype(jnp.float32) - (my_vp * vocab_rows).astype(jnp.float32)
@@ -349,6 +361,8 @@
             add(vocab_rows // PICK * PICK, vocab_rows % PICK)
 
     each_chunk(functools.partial(product, 1))
+    wait_peer_phase(1)
+    each_chunk(functools.partial(join, 1))
     pick_rows()
     for j in range(1, vp_size):
         share(e_src, e_in, row_sem.at[0], row_sem.at[1], "vp", j).start()
@@ -375,7 +389,8 @@
     wait_ring_phase(0)
     each_chunk(forward_chunk)
     each_chunk(functools.partial(product, 3))
-    nin_out[...] = _normalize(token_rows(), stat_total(1), norms[2], norms[3], full_width)
+    mean, rstd = _mean_rstd(stat_total(1), rows, full_width)
+    nin_out[...] = _normalize(token_rows(), mean, rstd, norms[2], norms[3])
 
     top[...] = jnp.full(top.shape, jnp.finfo(jnp.float32).min, jnp.float32)
     acc[...] = jnp.zeros_like(acc)
@@ -424,24 +439,27 @@
         new = functools.reduce(jnp.maximum, tops)
         return new, functools.reduce(jnp.add, [t * jnp.exp(b - new) for b, t in zip(tops, sums)])
 
-    stages = (("tp", far_first, lse_tp), ("vp", range(1, vp_size), lse_vp))
+    vp_far_first = sorted(range(1, vp_size), key=lambda j: -min(j, vp_size - j))
+    stages = (
+        ("tp", far_first, lse_in.at[pl.ds(0, tp_size - 1)]),
+        ("vp", vp_far_first, lse_in.at[pl.ds(tp_size - 1, vp_size - 1)]))
     for i, (axis, order, other) in enumerate(stages):
         lse_src[i, 0:1, :] = best
         lse_src[i, 1:2, :] = total
         for j in order:
-            share(lse_src.at[i], other, lse_sem.at[2 * i], lse_sem.at[2 * i + 1], axis, j).start()
-        all_shared(other, lse_sem.at[2 * i], lse_sem.at[2 * i + 1], axis).wait_recv()
+            share(lse_src.at[i], other, lse_send.at[0], lse_recv.at[i], axis, j).start()
+        all_shared(other, lse_send.at[0], lse_recv.at[i], axis).wait_recv()
         best, total = merge(best, total, other)
     ls_out[...] = jnp.broadcast_to(best + jnp.log(total), ls_out.shape)
 
-    for s in range(2):
-        all_shared(stat_in.at[s], stat_send.at[s], stat_recv.at[s], "tp").wait_send()
-    for i, (axis, _, other) in enumerate(stages):
-        all_shared(other, lse_sem.at[2 * i], lse_sem.at[2 * i + 1], axis).wait_send()
-    pltpu.make_async_remote_copy(
-        src_ref=mine, dst_ref=ring, send_sem=ring_send.at[0], recv_sem=ring_recv.at[0],
-        device_id={"tp": fwd}, device_id_type=MESH_ID).wait_send()
-    each_chunk(lambda k, last: [peer_copy(3, half, k, last).wait_send() for half in range(2)])
+    early_copy.wait_send()
+    all_shared(stat_in, stat_send.at[0], stat_recv.at[0], "tp").wait_send()
+    all_shared(lse_in, lse_send.at[0], lse_recv.at[0], "tp").wait_send()
+    sent_to_peer = to_peer.at[pl.ds(0, 4 * own_rows - 2 * buffer_rows(HEAD))]
+    for ref, sem in ((mine, ring_send), (sent_to_peer, peer_send)):
+        pltpu.make_async_remote_copy(
+            src_ref=ref, dst_ref=ref, send_sem=sem.at[0], recv_sem=ring_recv.at[0],
+            device_id={"tp": peer}, device_id_type=MESH_ID).wait_send()
 
 
 def _subtract_kernel(z, ls, nin, logprobs, log_sum, next_in, out, sums, sems):
@@ -502,9 +520,14 @@
                 pltpu.VMEM(emb_table.shape, emb_table.dtype),
                 pltpu.VMEM((3 * own_rows, LANES), f32),
                 pltpu.VMEM((4 * own_rows, LANES), f32),
-                pltpu.VMEM((n_chunks, rows * CHUNK // LANES, LANES), f32),
+                pltpu.VMEM((4 * own_rows, LANES), f32),
                 pltpu.VMEM((3 * own_rows, LANES), f32),
                 pltpu.VMEM((rows, width), jnp.bfloat16),
+                pltpu.VMEM((rows, width), jnp.bfloat16),
+                pltpu.VMEM((2 * HEAD, width), emb_table.dtype),
+                pltpu.VMEM((2 * HEAD + rows + 8, width), f32),
+                pltpu.VMEM((2 * HEAD + rows + 8, width), f32),
+                pltpu.VMEM((2 * HEAD, width), emb_table.dtype),
                 pltpu.VMEM((rows, LANES), f32),
                 pltpu.VMEM((rows, LANES), f32),
                 pltpu.VMEM((rows, width), f32),
@@ -512,23 +535,22 @@
                 pltpu.VMEM((2, 1, LANES), f32),
                 pltpu.VMEM((2, tp_size - 1, 1, LANES), f32),
                 pltpu.VMEM((2, 2, LANES), f32),
-                pltpu.VMEM((tp_size - 1, 2, LANES), f32),
-                pltpu.VMEM((vp_size - 1, 2, LANES), f32),
+                pltpu.VMEM((tp_size - 1 + vp_size - 1, 2, LANES), f32),
                 dma((3,)),
-                dma((4,)),
-                dma((n_chunks,)),
-                dma((2 * n_chunks + 2,)),
+                dma((2,)),
+                dma((3,)),
+                dma((1,)),
+                dma((n_chunks // 2 + 3,)),
                 dma((1,)),
                 dma((2 + n_chunks,)),
+                dma((1,)),
                 dma((2,)),
                 dma((2,)),
+                dma((1,)),
                 dma((2,)),
-                dma((2,)),
-                dma((2,)),
-                dma((4,)),
             ],
             compiler_params=pltpu.CompilerParams(
-                collective_id=0, has_side_effects=True, vmem_limit_bytes=58_000_000),
+                collective_id=0, has_side_effects=True, vmem_limit_bytes=64_500_000),
             name="vocab_head",
         )(
             hidden, lnf_gain.reshape(1, width), lnf_bias.reshape(1, width),

time: 87.7 us -> 86 us (0.981)
  Pallas kernels: 86.9 us -> 85.3 us
    pallas_call x1, Pallas kernels: 85.4 us -> 83.8 us  [per_device(): pl.pallas_call(functools.partial(_head_kernel, tp_size, vp_size), out_sha...]
where the time goes in v3:
time: 86 us; the launch traced here: 85.9 us
  Pallas kernels  85.3 us (99%)
    pallas_call x1, Pallas kernels, per_device(): pl.pallas_call(functools.partial(_head_kernel, tp_size, vp_size), out_sha...  83.8 us

profile of v3, /device:TPU:97, one launch (start us, length us, event | category | flops | bytes accessed | tf_op | source)
XLA Modules:
  0.0 85.9 jit_solution(2467605932143872017)
XLA Ops:
  0.6 83.8 %vocab_head.1 = (f32[3920,128]{1,0:T(8,128)S(1)}, f32[8,128]{1,0:T(8,128)S(1)}, bf16[64,256]{1,0:T(8,128)(2,1)S(1)}) custom-call(bf16[64,256]{1,0:T(8,128)(2,1)} %hid_hbm.1, f32[1,256]{1,0:T(1,128)} %bitcast.6, f32[1,256]{1,0:T(1,128)} %bitcast.7, f32[1,256]{1,0:T(1,128)} %bitcast.8, f32[1,256]{1,0:T(1,128)} %bitcast.9, s32[1,64]{1,0:T(1,128)} %bitcast.10, ...), custom_call_target="tpu_custom_call" | custom-call | tf_op jit(solution)/shard_map/vocab_head/pallas_call | solution.py:507
  84.5 1.5 %log_probs.1 = (f32[64,7840]{1,0:T(8,128)}, f32[1,64]{1,0:T(1,128)}, bf16[64,256]{1,0:T(8,128)(2,1)}) custom-call(f32[3920,128]{1,0:T(8,128)S(1)} %get-tuple-element.9.z, f32[8,128]{1,0:T(8,128)S(1)} %get-tuple-element.10.ls, bf16[64,256]{1,0:T(8,128)(2,1)S(1)} %get-tuple-element.11.nin), custom_call_target="tpu_custom_call" | custom-call | tf_op jit(solution)/shard_map/log_probs/pallas_call | solution.py:559

commit v4 on v3

--- a/solution.py
+++ b/solution.py
@@ -10,7 +10,8 @@
 NORM_EPS = 1e-5
 LANES = 128
 CHUNK = 1024
-HEAD = 384
+HEAD = 512
+HEAD_STEP = 128
 DOT_COLS = 512
 PICK = 1280
 MESH_ID = pl.DeviceIdType.MESH
@@ -57,7 +58,7 @@
     hid_hbm, g1_hbm, b1_hbm, g2_hbm, b2_hbm, tok_hbm, emb,
     z_out, ls_out, nin_out,
     hid, norms, tok,
-    e_all, mine, from_peer, to_peer, ring, xn, xn_peer, early, early_out, early_in, early_rows,
+    e_all, mine, from_peer, to_peer, ring, xn, xn_peer, early_out, early_in, early_rows,
     top, acc, e_src, e_in, stat_src, stat_in, lse_src, lse_in,
     small_sem, e_sem, early_sem, peer_send, peer_recv, ring_send, ring_recv,
     stat_send, stat_recv, row_sem, lse_send, lse_recv,
@@ -91,9 +92,12 @@
     bwd = 2 * chip_at(-turn) + core
 
     barrier = pltpu.get_barrier_semaphore()
-    far_first = sorted(range(1, tp_size), key=lambda j: -min(j, tp_size - j))
+    def tp_peer(j):
+        return 2 * chip_at(j // 2) + (core if j % 2 == 0 else 1 - core)
+
+    far_first = sorted(range(1, tp_size), key=lambda j: -min(j // 2, chips - j // 2))
     for j in far_first:
-        pl.semaphore_signal(barrier, inc=1, device_id={"tp": (me + j) % tp_size}, device_id_type=MESH_ID)
+        pl.semaphore_signal(barrier, inc=1, device_id={"tp": tp_peer(j)}, device_id_type=MESH_ID)
     for j in range(1, vp_size):
         pl.semaphore_signal(barrier, inc=1, device_id={"vp": (my_vp + j) % vp_size}, device_id_type=MESH_ID)
 
@@ -129,7 +133,7 @@
 
     for half in range(2):
         rows_at = pl.ds(pl.multiple_of(first_row(0, half, 0), 16), HEAD)
-        pltpu.make_async_copy(emb.at[rows_at], early.at[pl.ds(half * HEAD, HEAD)], early_sem.at[0]).start()
+        pltpu.make_async_copy(emb.at[rows_at], early_rows.at[pl.ds(half * HEAD, HEAD)], early_sem.at[0]).start()
 
     hid_load.wait()
     pltpu.make_async_copy(norms, norms, small_sem.at[2]).wait()
@@ -140,10 +144,10 @@
                 table_load(phase, half, own).start()
 
     def share(src, dst, send, recv, axis, j):
-        size, at = (tp_size, me) if axis == "tp" else (vp_size, my_vp)
+        to = tp_peer(j) if axis == "tp" else (my_vp + j) % vp_size
         return pltpu.make_async_remote_copy(
             src_ref=src, dst_ref=dst.at[j - 1], send_sem=send, recv_sem=recv,
-            device_id={axis: (at + j) % size}, device_id_type=MESH_ID)
+            device_id={axis: to}, device_id_type=MESH_ID)
 
     def all_shared(dst, send, recv, axis):
         at = (me + 1) % tp_size if axis == "tp" else (my_vp + 1) % vp_size
@@ -164,13 +168,13 @@
 
     x = hid[...].astype(jnp.float32)
     stat_src[0] = _row_stats(x)
+    pl.semaphore_wait(barrier, tp_size - 1 + vp_size - 1)
+    share_stats(0)
     early_out[pl.ds(2 * HEAD, rows), :] = x
     early_out[pl.ds(2 * HEAD + rows, 8), :] = jnp.concatenate(
         [norms[0], norms[1], jnp.zeros((6, width), jnp.float32)], axis=0)
-    pltpu.make_async_copy(emb.at[pl.ds(0, 2 * HEAD)], early, early_sem.at[0]).wait()
-    early_out[pl.ds(0, 2 * HEAD), :] = early[...].astype(jnp.float32)
-    pl.semaphore_wait(barrier, tp_size - 1 + vp_size - 1)
-    share_stats(0)
+    pltpu.make_async_copy(emb.at[pl.ds(0, 2 * HEAD)], early_rows, early_sem.at[0]).wait()
+    early_out[pl.ds(0, 2 * HEAD), :] = early_rows[...].astype(jnp.float32)
     early_copy = pltpu.make_async_remote_copy(
         src_ref=early_out, dst_ref=early_in, send_sem=early_sem.at[1], recv_sem=early_sem.at[2],
         device_id={"tp": peer}, device_id_type=MESH_ID)
@@ -253,10 +257,8 @@
             src_ref=ref, dst_ref=ref, send_sem=ring_send.at[0], recv_sem=ring_recv.at[phase],
             device_id={"tp": fwd}, device_id_type=MESH_ID).wait_recv()
 
-    head_rows = pl.ds(0, buffer_rows(HEAD))
-
-    def head_ring_copy(half):
-        span = pl.ds(half * half_chunks * buffer_rows(CHUNK), head_rows.size)
+    def head_ring_copy(half, c):
+        span = pl.ds(half * half_chunks * buffer_rows(CHUNK) + buffer_rows(c), buffer_rows(HEAD_STEP))
         return pltpu.make_async_remote_copy(
             src_ref=mine.at[span], dst_ref=ring.at[span],
             send_sem=ring_send.at[0], recv_sem=ring_recv.at[0],
@@ -281,15 +283,17 @@
         chunk_dot(dst, base, first_row(phase, half, 1) + k * CHUNK, first, end or cols_of(half, last))
 
     def first_product():
-        for half in range(2):
-            part = e_all[pl.ds(pl.multiple_of(first_row(0, half, 1), 16), HEAD), :]
-            dims = (((1,), (1,)), ((), ()))
-            v = lax.dot_general(xn[...], part, dims, preferred_element_type=jnp.float32) + lax.dot_general(
-                xn_peer[...], early_rows[pl.ds(half * HEAD, HEAD), :], dims, preferred_element_type=jnp.float32)
-            for t in range(0, HEAD, LANES):
-                mine[pl.ds(base_of(0, half, 0) + t // LANES * rows, rows), :] = v[:, t : t + LANES]
-        for half in range(2):
-            head_ring_copy(half).start()
+        dims = (((1,), (1,)), ((), ()))
+        for c in range(0, HEAD, HEAD_STEP):
+            for half in range(2):
+                part = e_all[pl.ds(pl.multiple_of(first_row(0, half, 1) + c, 16), HEAD_STEP), :]
+                v = lax.dot_general(xn[...], part, dims, preferred_element_type=jnp.float32) + lax.dot_general(
+                    xn_peer[...], early_rows[pl.ds(half * HEAD + c, HEAD_STEP), :], dims,
+                    preferred_element_type=jnp.float32)
+                for t in range(0, HEAD_STEP, LANES):
+                    mine[pl.ds(base_of(0, half, 0) + (c + t) // LANES * rows, rows), :] = v[:, t : t + LANES]
+            for half in range(2):
+                head_ring_copy(half, c).start()
         for half in range(2):
             to_peer_dot(0, half, 0, False, HEAD)
         for half in range(2):
@@ -524,7 +528,6 @@
                 pltpu.VMEM((3 * own_rows, LANES), f32),
                 pltpu.VMEM((rows, width), jnp.bfloat16),
                 pltpu.VMEM((rows, width), jnp.bfloat16),
-                pltpu.VMEM((2 * HEAD, width), emb_table.dtype),
                 pltpu.VMEM((2 * HEAD + rows + 8, width), f32),
                 pltpu.VMEM((2 * HEAD + rows + 8, width), f32),
                 pltpu.VMEM((2 * HEAD, width), emb_table.dtype),

time: 86 us -> 85.8 us (level)
  no operation moved by 1% of the time
where the time goes in v4:
time: 85.8 us; the launch traced here: 85.7 us
  Pallas kernels  85.1 us (99%)
    pallas_call x1, Pallas kernels, per_device(): pl.pallas_call(functools.partial(_head_kernel, tp_size, vp_size), out_sha...  83.6 us

profile of v4, /device:TPU:97, one launch (start us, length us, event | category | flops | bytes accessed | tf_op | source)
XLA Modules:
  0.0 85.7 jit_solution(12586818810933782958)
XLA Ops:
  0.6 83.6 %vocab_head.1 = (f32[3920,128]{1,0:T(8,128)S(1)}, f32[8,128]{1,0:T(8,128)S(1)}, bf16[64,256]{1,0:T(8,128)(2,1)S(1)}) custom-call(bf16[64,256]{1,0:T(8,128)(2,1)} %hid_hbm.1, f32[1,256]{1,0:T(1,128)} %bitcast.6, f32[1,256]{1,0:T(1,128)} %bitcast.7, f32[1,256]{1,0:T(1,128)} %bitcast.8, f32[1,256]{1,0:T(1,128)} %bitcast.9, s32[1,64]{1,0:T(1,128)} %bitcast.10, ...), custom_call_target="tpu_custom_call" | custom-call | tf_op jit(solution)/shard_map/vocab_head/pallas_call | solution.py:511
  84.3 1.5 %log_probs.1 = (f32[64,7840]{1,0:T(8,128)}, f32[1,64]{1,0:T(1,128)}, bf16[64,256]{1,0:T(8,128)(2,1)}) custom-call(f32[3920,128]{1,0:T(8,128)S(1)} %get-tuple-element.9.z, f32[8,128]{1,0:T(8,128)S(1)} %get-tuple-element.10.ls, bf16[64,256]{1,0:T(8,128)(2,1)S(1)} %get-tuple-element.11.nin), custom_call_target="tpu_custom_call" | custom-call | tf_op jit(solution)/shard_map/log_probs/pallas_call | solution.py:562

commit v5 on v4

--- a/solution.py
+++ b/solution.py
@@ -237,25 +237,28 @@
     def wait_peer_chunk(k, last):
         wait_peer(peer_recv_of(0, k), sum(span_of(0, half, k, last).size for half in range(2)))
 
-    def ring_recv_of(phase, half, k):
-        return ring_recv.at[phase if phase < 2 else 2 + half * half_chunks + k]
+    def ring_recv_of(phase, half, k, last):
+        return ring_recv.at[phase if phase < 2 else 2 + k + (half if last else 0)]
 
     def ring_copy(phase, half, k, last):
         span = span_of(phase, half, k, last)
         forward = (half == 0) != (phase == 1)
         return pltpu.make_async_remote_copy(
             src_ref=mine.at[span], dst_ref=ring.at[span],
-            send_sem=ring_send.at[0], recv_sem=ring_recv_of(phase, half, k),
+            send_sem=ring_send.at[0], recv_sem=ring_recv_of(phase, half, k, last),
             device_id={"tp": fwd if forward else bwd}, device_id_type=MESH_ID)
 
     def whole_phase(ref, phase):
         return ref.at[pl.ds(phase * own_rows, own_rows)]
 
+    def wait_ring(recv, count):
+        ref = ring.at[pl.ds(0, count)]
+        pltpu.make_async_remote_copy(
+            src_ref=ref, dst_ref=ref, send_sem=ring_send.at[0], recv_sem=recv,
+            device_id={"tp": fwd}, device_id_type=MESH_ID).wait_recv()
+
     def wait_ring_phase(phase):
-        ref = whole_phase(ring, phase)
-        pltpu.make_async_remote_copy(
-            src_ref=ref, dst_ref=ref, send_sem=ring_send.at[0], recv_sem=ring_recv.at[phase],
-            device_id={"tp": fwd}, device_id_type=MESH_ID).wait_recv()
+        wait_ring(ring_recv.at[phase], own_rows)
 
     def head_ring_copy(half, c):
         span = pl.ds(half * half_chunks * buffer_rows(CHUNK) + buffer_rows(c), buffer_rows(HEAD_STEP))
@@ -404,7 +407,10 @@
             cols = cols_of(half, last)
             base, peer_base = base_of(0, half, k), base_of(3, half, k)
             single, chain = base_of(1, half, k), base_of(2, half, k)
-            ring_copy(2, half, k, last).wait_recv()
+            if last:
+                ring_copy(2, half, k, last).wait_recv()
+            elif half == 0:
+                wait_ring(ring_recv_of(2, 0, k, False), 2 * buffer_rows(CHUNK))
 
             def final(r):
                 v = (z_out[pl.ds(base + r, 8), :] + from_peer[pl.ds(peer_base + r, 8), :]) + (
@@ -545,7 +551,7 @@
                 dma((1,)),
                 dma((n_chunks // 2 + 3,)),
                 dma((1,)),
-                dma((2 + n_chunks,)),
+                dma((2 + n_chunks // 2 + 1,)),
                 dma((1,)),
                 dma((2,)),
                 dma((2,)),

time: 85.8 us -> 85.8 us (level)
  no operation moved by 1% of the time
where the time goes in v5:
time: 85.8 us; the launch traced here: 85.7 us
  Pallas kernels  85.1 us (99%)
    pallas_call x1, Pallas kernels, per_device(): pl.pallas_call(functools.partial(_head_kernel, tp_size, vp_size), out_sha...  83.6 us

profile of v5, /device:TPU:97, one launch (start us, length us, event | category | flops | bytes accessed | tf_op | source)
XLA Modules:
  0.0 85.7 jit_solution(10415221705308918218)
XLA Ops:
  0.6 83.6 %vocab_head.1 = (f32[3920,128]{1,0:T(8,128)S(1)}, f32[8,128]{1,0:T(8,128)S(1)}, bf16[64,256]{1,0:T(8,128)(2,1)S(1)}) custom-call(bf16[64,256]{1,0:T(8,128)(2,1)} %hid_hbm.1, f32[1,256]{1,0:T(1,128)} %bitcast.6, f32[1,256]{1,0:T(1,128)} %bitcast.7, f32[1,256]{1,0:T(1,128)} %bitcast.8, f32[1,256]{1,0:T(1,128)} %bitcast.9, s32[1,64]{1,0:T(1,128)} %bitcast.10, ...), custom_call_target="tpu_custom_call" | custom-call | tf_op jit(solution)/shard_map/vocab_head/pallas_call | solution.py:517
  84.2 1.5 %log_probs.1 = (f32[64,7840]{1,0:T(8,128)}, f32[1,64]{1,0:T(1,128)}, bf16[64,256]{1,0:T(8,128)(2,1)}) custom-call(f32[3920,128]{1,0:T(8,128)S(1)} %get-tuple-element.9.z, f32[8,128]{1,0:T(8,128)S(1)} %get-tuple-element.10.ls, bf16[64,256]{1,0:T(8,128)(2,1)S(1)} %get-tuple-element.11.nin), custom_call_target="tpu_custom_call" | custom-call | tf_op jit(solution)/shard_map/log_probs/pallas_call | solution.py:568
